TPU v7x, 32 devices: a whole 2x2x4 slice. The times are simulated.
32 devices in a mesh: rep: 8 (over z, x), rows: 4 (over y, core).
Axes of the slice: x: 2, y: 2, z: 4, core: 2. Of those that a mesh axis runs over, the one named last changes fastest.
Arguments:
- item_table: bfloat16 [131072, 128], P(('rep', 'rows')), may hold values from -6 to 6
- history_ids: int32 [512, 64], P('rows'), may hold values from 0 to 131071, as said below
- history_mask: int32 [512, 64], P('rows'), may hold values 0 or 1
Outputs:
- user_vectors: float32 [512, 128], P('rows')
Inputs may be any that keep to these rules, and one draw needn't show every extreme that they name: `history_ids`: among the slots of the 128 bags of one index of rows (bags b * 128 to (b + 1) * 128 - 1), exactly 256 ids fall in each block of 4096 consecutive table rows, used or not.
All inputs are finite; a program needn't handle non-finite values. No bound on the sum of `history_mask` on one device may be relied on, other than what follows from the above.
Results may differ from a plain program's by a relative error of at most 0.0017.
Values may be sent and summed in bfloat16 or wider, within the bound.
No kernel may reach another device: no remote copies, remote signals or barrier semaphores. Data moves between devices by JAX's collectives and lax.ppermute only.
A program may use at most 128 MiB of HBM per device.

v0:
```python
import math

import jax
import jax.numpy as jnp
from jax import lax
from jax.sharding import PartitionSpec as P


def pool_rows(ids, mask, piece, offset):
    nbags, length = ids.shape
    block = math.gcd(nbags, 512)
    nhigh = piece.shape[0] // 128
    width = piece.shape[1]
    local = ids - offset
    high = jnp.floor_divide(local, 128)
    low = jnp.remainder(local, 128)

    def one_block(args):
        high_b, low_b, mask_b = args
        high_hot = (high_b[:, :, None] == jnp.arange(nhigh, dtype=jnp.int32)).astype(jnp.bfloat16)
        low_hot = (
            (low_b[:, :, None] == jnp.arange(128, dtype=jnp.int32)) & (mask_b[:, :, None] > 0)
        ).astype(jnp.bfloat16)
        counts = jnp.einsum("blh,blo->bho", high_hot, low_hot, preferred_element_type=jnp.float32)
        counts = counts.astype(jnp.bfloat16).reshape(block, nhigh * 128)
        return jnp.dot(counts, piece, preferred_element_type=jnp.float32)

    shaped = (
        high.reshape(-1, block, length),
        low.reshape(-1, block, length),
        mask.reshape(-1, block, length),
    )
    return lax.map(one_block, shaped).reshape(nbags, width)


def normalize(pooled):
    return pooled / jnp.sqrt(jnp.mean(pooled * pooled, axis=1, keepdims=True) + 1e-06)


def on_device(item_table, history_ids, history_mask):
    rows_dev = item_table.shape[0]
    group_size = lax.axis_size("rows")
    group_rows = rows_dev * group_size
    group_base = lax.axis_index("rep") * group_rows
    partial_value = pool_rows(
        history_ids,
        history_mask,
        lax.all_gather(item_table, "rows", axis=0, tiled=True),
        group_base,
    )
    pooled = lax.psum(partial_value, "rep")
    return normalize(pooled)


def solution(mesh):
    return jax.shard_map(
        on_device,
        mesh=mesh,
        in_specs=(P(("rep", "rows"), None), P("rows", None), P("rows", None)),
        out_specs=P("rows", None),
        check_vma=False,
    )
```

profile of v0, /device:TPU:0, one launch (start us, length us, event | category | flops | bytes accessed | tf_op | source)
XLA Modules:
  0.0 131.9 jit_solution(6185900074222709909)
XLA Ops:
  6.5 0.0 all-gather.2.cloned.1.call-start
  6.5 0.7 all-gather.2.cloned.1.call-update
  7.3 0.0 all-reduce.2.cloned.1.call-start
  7.3 0.8 add_select_fusion.1
  8.1 0.1 copy.4
  8.2 0.1 copy.5
  8.3 0.8 broadcast_compare_fusion
  9.1 0.1 copy.6
  9.2 10.8 %fusion.6 = bf16[128,128,128]{2,1,0:T(8,128)(2,1)} fusion(s32[128,64]{1,0:T(8,128)S(1)} %copy.5, s32[128,64]{1,0:T(8,128)S(1)} %copy.4, pred[128,64]{1,0:T(8,128)(4,1)S(1)} %copy.6), kind=kOutput, calls=%fused_computation.7 | convolution fusion | flops 273678336 | bytes 4268032 | tf_op jit(solution)/shard_map/while/body/eval_jaxpr/blh,blo->bho/dot_general | solution.py:24
  20.0 26.1 %all-gather.2.cloned.1.call-done = bf16[16384,128]{1,0:T(8,128)(2,1)} async-done(((bf16[4096,128]{1,0:T(8,128)(2,1)}), bf16[16384,128]{1,0:T(8,128)(2,1)}) %all-gather.2.cloned.1.call-update) | async-done | bytes 4194320 | tf_op jit(solution)/shard_map/all_gather | solution.py:48
  46.2 6.9 %fusion = f32[128,128]{1,0:T(8,128)} fusion(bf16[16384,128]{1,0:T(8,128)(2,1)} %all-gather.2.cloned.1.call-done, bf16[16,8,128,128]{3,2,1,0:T(8,128)(2,1)} %bitcast.5), kind=kOutput, calls=%fused_computation | convolution fusion | flops 536870912 | bytes 8454144 | tf_op jit(solution)/shard_map/while/body/eval_jaxpr/dot_general | solution.py:26
  53.0 0.0 all-reduce.2.cloned.1.call-update
  53.1 69.4 %all-reduce.2.cloned.1.call-done = f32[128,128]{1,0:T(8,128)} async-done(((f32[128,128]{1,0:T(8,128)}), f32[128,128]{1,0:T(8,128)}) %all-reduce.2.cloned.1.call-update) | async-done | bytes 65552 | tf_op jit(solution)/shard_map/psum | solution.py:51
  122.5 0.9 multiply_reduce_fusion
  123.5 1.6 %broadcast_divide_fusion = f32[128,128]{1,0:T(8,128)} fusion(f32[128,128]{1,0:T(8,128)} %all-reduce.2.cloned.1.call-done, f32[128]{0:T(128)S(1)} %add_sqrt_fusion), kind=kLoop, calls=%fused_computation.17 | loop fusion | flops 16384 | bytes 131584 | tf_op jit(solution)/shard_map/div | solution.py:37
  (1 shorter events, 0.0 us)
Async XLA Ops:
  6.5 39.6 %all-gather.2.cloned.1.call-start = ((), (), s32[]{:S(2)}) async-start(), calls=%async_computation | async-start | bytes 5242880 | tf_op jit(solution)/shard_map/all_gather | solution.py:48
  7.3 115.2 %all-reduce.2.cloned.1.call-start = ((), (), s32[]{:S(2)}) async-start(), calls=%async_computation.1 | async-start | bytes 131072 | tf_op jit(solution)/shard_map/psum | solution.py:51
Sparse Core Ops, SparseCore 0:
  8.9 37.2 all-gather.1
  53.2 69.2 all-reduce.1
where the time goes:
time: 132 us
  waiting for transfers between devices  96.3 us (73%)
  matrix products  17.7 us (13%)
  between operations  13.4 us (10%)
  other arithmetic  4.08 us (3%)
    psum x1, waiting for transfers between devices, on_device(): pooled = lax.psum(partial_value, 'rep')  69.4 us
    all_gather x1, waiting for transfers between devices, on_device(): lax.all_gather(item_table, 'rows', axis=0, tiled=True)  26.1 us
    dot_general x1, matrix products, one_block(): jnp.einsum('blh,blo->bho', high_hot, low_hot, preferred_element_type=jnp....  10.8 us
    dot_general x1, matrix products, one_block(): return jnp.dot(counts, piece, preferred_element_type=jnp.float32)  6.88 us
  transfers between devices with their start and end apart: 2, of which 2 were waited for; matrix products, arithmetic and copies ran while one was open for 10% of the time, Pallas kernels for 0%

commit v1 on v0

v1 whole, which is shorter than its diff:
```python
import functools

import jax
import jax.numpy as jnp
from jax import lax
from jax.experimental import pallas as pl
from jax.experimental.pallas import tpu as pltpu
from jax.sharding import PartitionSpec as P

LANES = 128
LOW = 256


def pool_kernel(base_ref, *refs, groups, highs, length, unroll):
    key_refs = refs[:groups]
    table_ref, out_ref, m_ref, low_ref, cnt0_ref, cnt1_ref = refs[groups:]
    per = LANES // length
    nbags = key_refs[0].shape[1]
    prow = nbags // per
    base = base_ref[0]
    lane = lax.broadcasted_iota(jnp.int32, (prow, LANES), 1)
    odd = lax.broadcasted_iota(jnp.int32, (prow, LANES), 0) & 1
    for g in range(groups):
        keys = jnp.concatenate([key_refs[g][...]] * per, axis=0).T
        packed = keys[:prow]
        for j in range(1, per):
            packed = jnp.where(lane >= j * length, keys[j * prow : (j + 1) * prow], packed)
        local = packed - base
        inside = (local >= 0) & (local < highs * LOW)
        m = lax.shift_right_arithmetic(local, LOW.bit_length() - 1) + highs * (lane // length + per * odd)
        m_ref[g * prow : (g + 1) * prow, :] = jnp.where(inside, m, -1).astype(jnp.float32)
        low_ref[g * prow : (g + 1) * prow, :] = jnp.where(inside, local & (LOW - 1), -1).astype(jnp.float32)

    def numbered(n):
        return lax.broadcasted_iota(jnp.int32, (n, LANES), 0).astype(jnp.float32).astype(jnp.bfloat16)

    iota_m, iota_low = numbered(2 * per * highs), numbered(LOW)
    one, zero = jnp.bfloat16(1), jnp.bfloat16(0)

    def hot(row, iota):
        row = jnp.broadcast_to(row, (16, LANES)).astype(jnp.bfloat16)
        tiles = [jnp.where(iota[k : k + 16] == row, one, zero) for k in range(0, iota.shape[0], 16)]
        return jnp.concatenate(tiles, axis=0)

    def step(c, carry):
        for u in range(unroll):
            p = (c * unroll + u) * 2
            pair = [pl.ds(p, 1), pl.ds(p + 1, 1)]
            lhs = jnp.concatenate([hot(m_ref[at, :], iota_m) for at in pair], axis=1)
            rhs = jnp.concatenate([hot(low_ref[at, :], iota_low) for at in pair], axis=1)
            cnt = lax.dot_general(lhs, rhs, (((1,), (1,)), ((), ())), preferred_element_type=jnp.float32)
            g = p // prow
            for i in range(2 * per):
                bag = g * nbags + (i % per) * prow + (p - g * prow) + i // per
                at = pl.ds(pl.multiple_of(bag * highs, highs), highs)
                cnt0_ref[at, :] = cnt[i * highs : (i + 1) * highs, :LANES]
                cnt1_ref[at, :] = cnt[i * highs : (i + 1) * highs, LANES:]
        return carry

    lax.fori_loop(0, groups * prow // 2 // unroll, step, 0)
    total = groups * nbags
    acc = jnp.zeros((total, table_ref.shape[1]), jnp.float32)
    for h in range(highs):
        at = pl.ds(h, total, stride=highs)
        counts = jnp.concatenate([cnt0_ref[at, :].astype(jnp.bfloat16), cnt1_ref[at, :].astype(jnp.bfloat16)], axis=1)
        acc += jnp.dot(counts, table_ref[h * LOW : (h + 1) * LOW, :], preferred_element_type=jnp.float32)
    out_ref[...] = acc.reshape(groups, nbags, table_ref.shape[1])


def pool(base, keys, table):
    groups, (length, nbags), (rows, width) = len(keys), keys[0].shape, table.shape
    highs, total = rows // LOW, groups * nbags
    vmem = pl.BlockSpec(memory_space=pltpu.VMEM)
    lanes = pltpu.VMEM((total * length // LANES, LANES), jnp.float32)
    counts = pltpu.VMEM((total * highs, LANES), jnp.float32)
    return pl.pallas_call(
        functools.partial(pool_kernel, groups=groups, highs=highs, length=length, unroll=8),
        out_shape=jax.ShapeDtypeStruct((groups, nbags, width), jnp.float32),
        in_specs=[pl.BlockSpec(memory_space=pltpu.SMEM)] + [vmem] * (groups + 1),
        out_specs=vmem,
        scratch_shapes=[lanes, lanes, counts, counts],
        cost_estimate=pl.CostEstimate(
            flops=4 * total * rows * width, bytes_accessed=rows * width * 2, transcendentals=0
        ),
        compiler_params=pltpu.CompilerParams(vmem_limit_bytes=40 << 20),
    )(base, *keys, table)


def swap(value, axis, size, bit):
    return lax.ppermute(value, axis, [(i, i ^ bit) for i in range(size)])


def on_device(rows_size, rep_size, item_table, history_ids, history_mask):
    rows_dev = item_table.shape[0]
    block = lax.axis_index("rep") * rows_size + lax.axis_index("rows")
    base = (block * rows_dev).astype(jnp.int32).reshape(1)
    key = jnp.where(history_mask > 0, history_ids, -1).T
    keys = [key] + [swap(key, "rows", rows_size, s) for s in range(1, rows_size)]
    near = pool(base, keys[:2], item_table)
    sums = [near[0], near[1]]
    mine = sums[0] + swap(sums[1], "rows", rows_size, 1)
    far = []
    for s in range(2, rows_size, 2):
        part = pool(base, keys[s : s + 2], item_table)
        far.append(part[0] + swap(part[1], "rows", rows_size, 1))
    sums = [mine] + far
    while len(sums) > 1:
        half = len(sums) // 2
        sums = [a + swap(b, "rows", rows_size, 2 * half) for a, b in zip(sums[:half], sums[half:])]
    pooled = sums[0]
    bit = 1
    while bit < rep_size:
        pooled = pooled + swap(pooled, "rep", rep_size, bit)
        bit *= 2
    return pooled / jnp.sqrt(jnp.mean(pooled * pooled, axis=1, keepdims=True) + 1e-06)


def solution(mesh):
    body = functools.partial(on_device, mesh.shape["rows"], mesh.shape["rep"])
    return jax.shard_map(
        body,
        mesh=mesh,
        in_specs=(P(("rep", "rows"), None), P("rows", None), P("rows", None)),
        out_specs=P("rows", None),
        check_vma=False,
    )
```

time: 132 us -> 38.9 us (0.29)
  waiting for transfers between devices: 96.3 us -> 14.7 us
  matrix products: 17.7 us -> 0 us
  between operations: 13.4 us -> 0.09 us
  starting transfers between devices: 0.04 us -> 10.7 us
  Pallas kernels: 0 us -> 10.2 us
  other arithmetic: 4.08 us -> 1.66 us
    psum x1 -> x0, waiting for transfers between devices: 69.4 us -> none  [on_device(): pooled = lax.psum(partial_value, 'rep')]
    all_gather x1 -> x0, waiting for transfers between devices: 26.1 us -> none  [on_device(): lax.all_gather(item_table, 'rows', axis=0, tiled=True)]
    dot_general x2 -> x0, matrix products: 17.7 us -> none  [the longest x1 10.8 us: one_block(): jnp.einsum('blh,blo->bho', high_hot, low_hot, preferred_element_type=jnp....]
    ppermute x0 -> x9, waiting for transfers between devices: none -> 14.7 us  [swap(): return lax.ppermute(value, axis, [(i, i ^ bit) for i in range(size)])]
    ppermute x0 -> x9, starting transfers between devices: none -> 10.7 us  [swap(): return lax.ppermute(value, axis, [(i, i ^ bit) for i in range(size)])]
    pallas_call x0 -> x2, Pallas kernels: none -> 10.2 us  [pool(): pl.pallas_call(functools.partial(pool_kernel, groups=groups, highs=highs,...]
  transfers between devices with their start and end apart: 2 -> 9, of which waited for: 2 -> 7; matrix products, arithmetic and copies ran while one was open for 10% -> 0% of each run, Pallas kernels for 0% -> 26%
where the time goes in v1:
time: 38.9 us; the launch traced here: 38.7 us
  waiting for transfers between devices  14.7 us (38%)
  starting transfers between devices  10.7 us (28%)
  Pallas kernels  10.2 us (26%)
  other arithmetic  1.66 us (4%)
  local copies, waits for them, and re-layouts  1.24 us (3%)
    ppermute x9, waiting for transfers between devices, swap(): return lax.ppermute(value, axis, [(i, i ^ bit) for i in range(size)])  14.7 us
    ppermute x9, starting transfers between devices, swap(): return lax.ppermute(value, axis, [(i, i ^ bit) for i in range(size)])  10.7 us
    pallas_call x2, Pallas kernels, pool(): pl.pallas_call(functools.partial(pool_kernel, groups=groups, highs=highs,...  10.2 us
    unnamed x4, local copies, waits for them, and re-layouts  1.23 us
    transpose x1, other arithmetic, on_device(): key = jnp.where(history_mask > 0, history_ids, -1).T  0.78 us
  transfers between devices with their start and end apart: 9, of which 7 were waited for; matrix products, arithmetic and copies ran while one was open for 0% of the time, Pallas kernels for 26%

profile of v1, /device:TPU:0, one launch (start us, length us, event | category | flops | bytes accessed | tf_op | source)
XLA Modules:
  0.0 38.7 jit_solution(8307474480376839822)
XLA Ops:
  0.0 0.8 %select_bitcast_fusion.refs_0_ = s32[64,128]{1,0:T(8,128)S(1)} fusion(s32[128,64]{0,1:T(8,128)} %param.4, s32[128,64]{0,1:T(8,128)} %param.5), kind=kLoop, calls=%fused_computation.9 | loop fusion | flops 16384 | bytes 98304 | tf_op jit(solution)/shard_map/transpose | solution.py:97
  0.8 3.0 %collective-permute-start.2 = (s32[64,128]{1,0:T(8,128)S(1)}, s32[64,128]{1,0:T(8,128)S(1)}, u32[]{:S(2)}, u32[]{:S(2)}) collective-permute-start(s32[64,128]{1,0:T(8,128)S(1)} %select_bitcast_fusion.refs_0_), channel_id=1, source_target_pairs={{0,2},{1,3},{2,0},{3,1},{4,6},{5,7},{6,4},{7,5},{8,10},{9,11},{10,... | collective-permute-start | bytes 98312 | tf_op jit(solution)/shard_map/ppermute | solution.py:90
  3.8 0.0 collective-permute-start.3
  3.8 0.2 collective-permute-start
  4.0 1.7 %collective-permute-done.2.refs_0_ = s32[64,128]{1,0:T(8,128)S(1)} collective-permute-done((s32[64,128]{1,0:T(8,128)S(1)}, s32[64,128]{1,0:T(8,128)S(1)}, u32[]{:S(2)}, u32[]{:S(2)}) %collective-permute-start.2) | collective-permute-done | bytes 32800 | tf_op jit(solution)/shard_map/ppermute | solution.py:90
  5.7 1.5 %collective-permute-done.3.refs_1_ = s32[64,128]{1,0:T(8,128)S(1)} collective-permute-done((s32[64,128]{1,0:T(8,128)S(1)}, s32[64,128]{1,0:T(8,128)S(1)}, u32[]{:S(2)}, u32[]{:S(2)}) %collective-permute-start.3) | collective-permute-done | bytes 32800 | tf_op jit(solution)/shard_map/ppermute | solution.py:90
  7.2 1.2 %copy-done = bf16[4096,128]{1,0:T(8,128)(2,1)S(1)} copy-done((bf16[4096,128]{1,0:T(8,128)(2,1)S(1)}, bf16[4096,128]{1,0:T(8,128)(2,1)}, u32[]{:S(2)}) %copy-start) | copy-done | bytes 1048600
  8.4 5.1 %shard_map.38 = f32[2,128,128]{2,1,0:T(8,128)S(1)} custom-call(s32[1]{0:T(128)} %bitcast.base_ref, s32[64,128]{1,0:T(8,128)S(1)} %collective-permute-done.2.refs_0_, s32[64,128]{1,0:T(8,128)S(1)} %collective-permute-done.3.refs_1_, bf16[4096,128]{1,0:T(8,128)(2,1)S(1)} %copy-done), custom_call_target="tpu_custom_call" | custom-call | flops 536870912 | bytes 1048576 | tf_op jit(solution)/shard_map/pallas_call | solution.py:76
  13.6 0.1 collective-permute-start.4
  13.7 0.0 collective-permute-done.refs_1_
  13.7 5.1 %shard_map.37 = f32[2,128,128]{2,1,0:T(8,128)S(1)} custom-call(s32[1]{0:T(128)} %bitcast.base_ref, s32[64,128]{1,0:T(8,128)S(1)} %select_bitcast_fusion.refs_0_, s32[64,128]{1,0:T(8,128)S(1)} %collective-permute-done.refs_1_, bf16[4096,128]{1,0:T(8,128)(2,1)S(1)} %copy-done.1), custom_call_target="tpu_custom_call" | custom-call | flops 536870912 | bytes 1048576 | tf_op jit(solution)/shard_map/pallas_call | solution.py:76
  18.8 0.6 %collective-permute-start.1 = (f32[128,128]{1,0:T(8,128)S(1)}, f32[128,128]{1,0:T(8,128)S(1)}, u32[]{:S(2)}, u32[]{:S(2)}) collective-permute-start(f32[128,128]{1,0:T(8,128)S(1)} %slice_bitcast_fusion.2), channel_id=1, source_target_pairs={{0,1},{1,0},{2,3},{3,2},{4,5},{5,4},{6,7},{7,6},{8,9},{9,8},{10,11... | collective-permute-start | bytes 196616 | tf_op jit(solution)/shard_map/ppermute | solution.py:90
  19.4 0.0 collective-permute-done.4
  19.4 0.6 %collective-permute-start.5 = (f32[128,128]{1,0:T(8,128)S(1)}, f32[128,128]{1,0:T(8,128)S(1)}, u32[]{:S(2)}, u32[]{:S(2)}) collective-permute-start(f32[128,128]{1,0:T(8,128)S(1)} %fusion), channel_id=1, source_target_pairs={{0,2},{1,3},{2,0},{3,1},{4,6},{5,7},{6,4},{7,5},{8,10},{9,11},{10,... | collective-permute-start | bytes 196616 | tf_op jit(solution)/shard_map/ppermute | solution.py:90
  19.9 0.3 collective-permute-done.1
  20.3 3.4 %collective-permute-done.5 = f32[128,128]{1,0:T(8,128)S(1)} collective-permute-done((f32[128,128]{1,0:T(8,128)S(1)}, f32[128,128]{1,0:T(8,128)S(1)}, u32[]{:S(2)}, u32[]{:S(2)}) %collective-permute-start.5) | collective-permute-done | bytes 65568 | tf_op jit(solution)/shard_map/ppermute | solution.py:90
  23.7 1.6 %collective-permute-start.6 = (f32[128,128]{1,0:T(8,128)S(1)}, f32[128,128]{1,0:T(8,128)S(1)}, u32[]{:S(2)}, u32[]{:S(2)}) collective-permute-start(f32[128,128]{1,0:T(8,128)S(1)} %fusion.2), channel_id=1, source_target_pairs={{0,4},{4,0},{8,12},{12,8},{16,20},{20,16},{24,28},{28,24},{1,5},{5... | collective-permute-start | bytes 196616 | tf_op jit(solution)/shard_map/ppermute | solution.py:90
  25.3 2.8 %collective-permute-done.6 = f32[128,128]{1,0:T(8,128)S(1)} collective-permute-done((f32[128,128]{1,0:T(8,128)S(1)}, f32[128,128]{1,0:T(8,128)S(1)}, u32[]{:S(2)}, u32[]{:S(2)}) %collective-permute-start.6) | collective-permute-done | bytes 65568 | tf_op jit(solution)/shard_map/ppermute | solution.py:90
  28.1 1.6 %collective-permute-start.7 = (f32[128,128]{1,0:T(8,128)S(1)}, f32[128,128]{1,0:T(8,128)S(1)}, u32[]{:S(2)}, u32[]{:S(2)}) collective-permute-start(f32[128,128]{1,0:T(8,128)S(1)} %add.36), channel_id=1, source_target_pairs={{0,8},{4,12},{8,0},{12,4},{16,24},{20,28},{24,16},{28,20},{1,9},{5... | collective-permute-start | bytes 196616 | tf_op jit(solution)/shard_map/ppermute | solution.py:90
  29.7 2.7 %collective-permute-done.7 = f32[128,128]{1,0:T(8,128)S(1)} collective-permute-done((f32[128,128]{1,0:T(8,128)S(1)}, f32[128,128]{1,0:T(8,128)S(1)}, u32[]{:S(2)}, u32[]{:S(2)}) %collective-permute-start.7) | collective-permute-done | bytes 65568 | tf_op jit(solution)/shard_map/ppermute | solution.py:90
  32.4 3.2 %collective-permute-start.8 = (f32[128,128]{1,0:T(8,128)S(1)}, f32[128,128]{1,0:T(8,128)S(1)}, u32[]{:S(2)}, u32[]{:S(2)}) collective-permute-start(f32[128,128]{1,0:T(8,128)S(1)} %add.37), channel_id=1, source_target_pairs={{0,16},{4,20},{8,24},{12,28},{16,0},{20,4},{24,8},{28,12},{1,17},{... | collective-permute-start | bytes 196616 | tf_op jit(solution)/shard_map/ppermute | solution.py:90
  35.6 2.2 %collective-permute-done.8 = f32[128,128]{1,0:T(8,128)S(1)} collective-permute-done((f32[128,128]{1,0:T(8,128)S(1)}, f32[128,128]{1,0:T(8,128)S(1)}, u32[]{:S(2)}, u32[]{:S(2)}) %collective-permute-start.8) | collective-permute-done | bytes 65568 | tf_op jit(solution)/shard_map/ppermute | solution.py:90
  37.9 0.1 multiply_reduce_fusion
  38.0 0.7 %broadcast_divide_fusion = f32[128,128]{1,0:T(8,128)} fusion(f32[128,128]{1,0:T(8,128)S(1)} %get-tuple-element.6, f32[128]{0:T(128)S(1)} %add_sqrt_fusion), kind=kLoop, calls=%fused_computation.8 | loop fusion | flops 16384 | bytes 131584 | tf_op jit(solution)/shard_map/div | solution.py:115
  (10 shorter events, 0.1 us)
Async XLA Ops:
  0.8 4.9 %collective-permute-start.2 = (s32[64,128]{1,0:T(8,128)S(1)}, s32[64,128]{1,0:T(8,128)S(1)}, u32[]{:S(2)}, u32[]{:S(2)}) collective-permute-start(s32[64,128]{1,0:T(8,128)S(1)} %select_bitcast_fusion.refs_0_), channel_id=1, source_target_pairs={{0,2},{1,3},{2,0},{3,1},{4,6},{5,7},{6,4},{7,5},{8,10},{9,11},{10,... | collective-permute-start | bytes 98312 | tf_op jit(solution)/shard_map/ppermute | solution.py:90
  3.8 3.4 %collective-permute-start.3 = (s32[64,128]{1,0:T(8,128)S(1)}, s32[64,128]{1,0:T(8,128)S(1)}, u32[]{:S(2)}, u32[]{:S(2)}) collective-permute-start(s32[64,128]{1,0:T(8,128)S(1)} %select_bitcast_fusion.refs_0_), channel_id=1, source_target_pairs={{0,3},{1,2},{2,1},{3,0},{4,7},{5,6},{6,5},{7,4},{8,11},{9,10},{10,... | collective-permute-start | bytes 98312 | tf_op jit(solution)/shard_map/ppermute | solution.py:90
  3.8 9.9 %collective-permute-start = (s32[64,128]{1,0:T(8,128)S(1)}, s32[64,128]{1,0:T(8,128)S(1)}, u32[]{:S(2)}, u32[]{:S(2)}) collective-permute-start(s32[64,128]{1,0:T(8,128)S(1)} %select_bitcast_fusion.refs_0_), channel_id=1, source_target_pairs={{0,1},{1,0},{2,3},{3,2},{4,5},{5,4},{6,7},{7,6},{8,9},{9,8},{10,11... | collective-permute-start | bytes 98312 | tf_op jit(solution)/shard_map/ppermute | solution.py:90
  7.2 1.2 %copy-start = (bf16[4096,128]{1,0:T(8,128)(2,1)S(1)}, bf16[4096,128]{1,0:T(8,128)(2,1)}, u32[]{:S(2)}) copy-start(bf16[4096,128]{1,0:T(8,128)(2,1)} %refs_2_.3) | copy-start | bytes 3145732
  8.4 5.2 %copy-start.1 = (bf16[4096,128]{1,0:T(8,128)(2,1)S(1)}, bf16[4096,128]{1,0:T(8,128)(2,1)}, u32[]{:S(2)}) copy-start(bf16[4096,128]{1,0:T(8,128)(2,1)} %refs_2_.3) | copy-start | bytes 3145732
  13.6 5.8 %collective-permute-start.4 = (f32[128,128]{1,0:T(8,128)S(1)}, f32[128,128]{1,0:T(8,128)S(1)}, u32[]{:S(2)}, u32[]{:S(2)}) collective-permute-start(f32[128,128]{1,0:T(8,128)S(1)} %slice_bitcast_fusion), channel_id=1, source_target_pairs={{0,1},{1,0},{2,3},{3,2},{4,5},{5,4},{6,7},{7,6},{8,9},{9,8},{10,11... | collective-permute-start | bytes 196616 | tf_op jit(solution)/shard_map/ppermute | solution.py:90
  18.8 1.5 %collective-permute-start.1 = (f32[128,128]{1,0:T(8,128)S(1)}, f32[128,128]{1,0:T(8,128)S(1)}, u32[]{:S(2)}, u32[]{:S(2)}) collective-permute-start(f32[128,128]{1,0:T(8,128)S(1)} %slice_bitcast_fusion.2), channel_id=1, source_target_pairs={{0,1},{1,0},{2,3},{3,2},{4,5},{5,4},{6,7},{7,6},{8,9},{9,8},{10,11... | collective-permute-start | bytes 196616 | tf_op jit(solution)/shard_map/ppermute | solution.py:90
  19.4 4.3 %collective-permute-start.5 = (f32[128,128]{1,0:T(8,128)S(1)}, f32[128,128]{1,0:T(8,128)S(1)}, u32[]{:S(2)}, u32[]{:S(2)}) collective-permute-start(f32[128,128]{1,0:T(8,128)S(1)} %fusion), channel_id=1, source_target_pairs={{0,2},{1,3},{2,0},{3,1},{4,6},{5,7},{6,4},{7,5},{8,10},{9,11},{10,... | collective-permute-start | bytes 196616 | tf_op jit(solution)/shard_map/ppermute | solution.py:90
  23.7 4.3 %collective-permute-start.6 = (f32[128,128]{1,0:T(8,128)S(1)}, f32[128,128]{1,0:T(8,128)S(1)}, u32[]{:S(2)}, u32[]{:S(2)}) collective-permute-start(f32[128,128]{1,0:T(8,128)S(1)} %fusion.2), channel_id=1, source_target_pairs={{0,4},{4,0},{8,12},{12,8},{16,20},{20,16},{24,28},{28,24},{1,5},{5... | collective-permute-start | bytes 196616 | tf_op jit(solution)/shard_map/ppermute | solution.py:90
  28.1 4.3 %collective-permute-start.7 = (f32[128,128]{1,0:T(8,128)S(1)}, f32[128,128]{1,0:T(8,128)S(1)}, u32[]{:S(2)}, u32[]{:S(2)}) collective-permute-start(f32[128,128]{1,0:T(8,128)S(1)} %add.36), channel_id=1, source_target_pairs={{0,8},{4,12},{8,0},{12,4},{16,24},{20,28},{24,16},{28,20},{1,9},{5... | collective-permute-start | bytes 196616 | tf_op jit(solution)/shard_map/ppermute | solution.py:90
  32.4 5.4 %collective-permute-start.8 = (f32[128,128]{1,0:T(8,128)S(1)}, f32[128,128]{1,0:T(8,128)S(1)}, u32[]{:S(2)}, u32[]{:S(2)}) collective-permute-start(f32[128,128]{1,0:T(8,128)S(1)} %add.37), channel_id=1, source_target_pairs={{0,16},{4,20},{8,24},{12,28},{16,0},{20,4},{24,8},{28,12},{1,17},{... | collective-permute-start | bytes 196616 | tf_op jit(solution)/shard_map/ppermute | solution.py:90

commit v2 on v1

v2 whole, which is shorter than its diff:
```python
import functools

import jax
import jax.numpy as jnp
from jax import lax
from jax.experimental import pallas as pl
from jax.experimental.pallas import tpu as pltpu
from jax.sharding import PartitionSpec as P

LANES = 128
GAP = 4


def pool_kernel(key_ref, own_hbm, other_ref, out_ref, own_ref, m_ref, low_ref, cnt_ref, sem, *, highs):
    load = pltpu.make_async_copy(own_hbm, own_ref, sem)
    load.start()
    length, nbags = key_ref.shape
    per = LANES // length
    prow = nbags // per
    lane = lax.broadcasted_iota(jnp.int32, (prow, LANES), 1)
    odd = lax.broadcasted_iota(jnp.int32, (prow, LANES), 0) & 1
    keys = jnp.concatenate([key_ref[...]] * per, axis=0).T
    local = keys[:prow]
    for j in range(1, per):
        local = jnp.where(lane >= j * length, keys[j * prow : (j + 1) * prow], local)
    m = lax.shift_right_arithmetic(local, LANES.bit_length() - 1) + highs * (lane // length + per * odd)
    m_ref[...] = jnp.where(local >= 0, m, -1).astype(jnp.float32)
    low_ref[...] = (local & (LANES - 1)).astype(jnp.float32)
    pitch = nbags + GAP
    nums = lax.broadcasted_iota(jnp.int32, (max(2 * per * highs, LANES), LANES), 0)
    nums = nums.astype(jnp.float32).astype(jnp.bfloat16)
    one, zero = jnp.bfloat16(1), jnp.bfloat16(0)

    def hot(row, n):
        row = jnp.broadcast_to(row, (16, LANES)).astype(jnp.bfloat16)
        return jnp.concatenate([jnp.where(nums[k : k + 16] == row, one, zero) for k in range(0, n, 16)], axis=0)

    for p in range(0, prow, 2):
        lhs = jnp.concatenate([hot(m_ref[k : k + 1, :], 2 * per * highs) for k in (p, p + 1)], axis=1)
        rhs = jnp.concatenate([hot(low_ref[k : k + 1, :], LANES) for k in (p, p + 1)], axis=1)
        cnt = lax.dot_general(lhs, rhs, (((1,), (1,)), ((), ())), preferred_element_type=jnp.float32)
        for i in range(2 * per):
            bag = (i % per) * prow + p + i // per
            for h in range(0, highs, 8):
                cnt_ref[pl.ds(h * pitch + bag, 8, stride=pitch), :] = cnt[i * highs + h : i * highs + h + 8, :]
    acc = jnp.zeros(out_ref.shape, jnp.float32)
    load.wait()
    for h in range(0, highs, 2):
        counts = [cnt_ref[k * pitch : k * pitch + nbags, :].astype(jnp.bfloat16) for k in (h, h + 1)]
        table, at = (own_ref, h) if 2 * h < highs else (other_ref, h - highs // 2)
        rows = table[at * LANES : (at + 2) * LANES, :]
        acc += jnp.dot(jnp.concatenate(counts, axis=1), rows, preferred_element_type=jnp.float32)
    out_ref[...] = acc


def pool(key, own, other):
    (length, nbags), (rows, width) = key.shape, own.shape
    highs = 2 * rows // LANES
    vmem = pl.BlockSpec(memory_space=pltpu.VMEM)
    packed = pltpu.VMEM((nbags * length // LANES, LANES), jnp.float32)
    return pl.pallas_call(
        functools.partial(pool_kernel, highs=highs),
        out_shape=jax.ShapeDtypeStruct((nbags, width), jnp.float32),
        in_specs=[vmem, pl.BlockSpec(memory_space=pltpu.HBM), vmem],
        out_specs=vmem,
        scratch_shapes=[
            pltpu.VMEM(own.shape, own.dtype),
            packed,
            packed,
            pltpu.VMEM((highs * (nbags + GAP), LANES), jnp.float32),
            pltpu.SemaphoreType.DMA,
        ],
        cost_estimate=pl.CostEstimate(
            flops=8 * nbags * rows * width, bytes_accessed=rows * width * 4, transcendentals=0
        ),
        compiler_params=pltpu.CompilerParams(vmem_limit_bytes=32 << 20),
    )(key, own, other)


def swap(value, axis, size, bit):
    return lax.ppermute(value, axis, [(i, i ^ bit) for i in range(size)])


def on_device(rows_size, rep_size, item_table, history_ids, history_mask):
    rows_dev = item_table.shape[0]
    other = swap(item_table, "rows", rows_size, 1)
    row, rep = lax.axis_index("rows"), lax.axis_index("rep")

    def key_for(s):
        there = row ^ s
        local = history_ids - (rep * rows_size + (there & -2)) * rows_dev
        used = (history_mask > 0) & (local >= 0) & (local < 2 * rows_dev)
        return jnp.where(used, local ^ ((there & 1) * rows_dev), -1).T

    keys = [swap(key_for(s), "rows", rows_size, s) for s in range(2, rows_size, 2)]
    near = pool(key_for(0), item_table, other)
    keys, near = lax.optimization_barrier((keys, near))
    sums = [near] + [pool(k, item_table, other) for k in keys]
    while len(sums) > 1:
        half = len(sums) // 2
        sums = [a + swap(b, "rows", rows_size, 2 * half) for a, b in zip(sums[:half], sums[half:])]
    pooled = sums[0]
    bit = 1
    while bit < rep_size:
        pooled = pooled + swap(pooled, "rep", rep_size, bit)
        bit *= 2
    return pooled / jnp.sqrt(jnp.mean(pooled * pooled, axis=1, keepdims=True) + 1e-06)


def solution(mesh):
    body = functools.partial(on_device, mesh.shape["rows"], mesh.shape["rep"])
    return jax.shard_map(
        body,
        mesh=mesh,
        in_specs=(P(("rep", "rows"), None), P("rows", None), P("rows", None)),
        out_specs=P("rows", None),
        check_vma=False,
    )
```

time: 38.9 us -> 29.6 us (0.76)
  Pallas kernels: 10.2 us -> 4.28 us
  waiting for transfers between devices: 14.7 us -> 10.8 us
  starting transfers between devices: 10.7 us -> 11.1 us
    pallas_call x2, Pallas kernels: 10.2 us -> 4.28 us  [pool(): pl.pallas_call(functools.partial(pool_kernel, highs=highs), out_shape=jax...]
    ppermute x9 -> x6, waiting for transfers between devices: 14.7 us -> 10.8 us  [swap(): return lax.ppermute(value, axis, [(i, i ^ bit) for i in range(size)])]
    ppermute x9 -> x6, starting transfers between devices: 10.7 us -> 11.1 us  [swap(): return lax.ppermute(value, axis, [(i, i ^ bit) for i in range(size)])]
    unnamed x4 -> x6, local copies, waits for them, and re-layouts: 1.23 us -> 1.49 us
    transpose x1 -> x2, other arithmetic: 0.78 us -> 0.8 us  [key_for(): return jnp.where(used, local ^ (there & 1) * rows_dev, -1).T]
  transfers between devices with their start and end apart: 9 -> 6, of which waited for: 7 -> 4; matrix products, arithmetic and copies ran while one was open for 0% -> 3% of each run, Pallas kernels for 26% -> 7%
where the time goes in v2:
time: 29.6 us; the launch traced here: 29.3 us
  starting transfers between devices  11.1 us (38%)
  waiting for transfers between devices  10.8 us (36%)
  Pallas kernels  4.28 us (14%)
  other arithmetic  1.67 us (6%)
  local copies, waits for them, and re-layouts  1.49 us (5%)
    ppermute x6, starting transfers between devices, swap(): return lax.ppermute(value, axis, [(i, i ^ bit) for i in range(size)])  11.1 us
    ppermute x6, waiting for transfers between devices, swap(): return lax.ppermute(value, axis, [(i, i ^ bit) for i in range(size)])  10.8 us
    pallas_call x2, Pallas kernels, pool(): pl.pallas_call(functools.partial(pool_kernel, highs=highs), out_shape=jax...  4.28 us
    unnamed x6, local copies, waits for them, and re-layouts  1.49 us
    transpose x2, other arithmetic, key_for(): return jnp.where(used, local ^ (there & 1) * rows_dev, -1).T  0.8 us
    div x1, other arithmetic, on_device(): pooled / jnp.sqrt(jnp.mean(pooled * pooled, axis=1, keepdims=True) + 1e-06)  0.73 us
  transfers between devices with their start and end apart: 6, of which 4 were waited for; matrix products, arithmetic and copies ran while one was open for 3% of the time, Pallas kernels for 7%

profile of v2, /device:TPU:0, one launch (start us, length us, event | category | flops | bytes accessed | tf_op | source)
XLA Modules:
  0.0 29.3 jit_solution(15796968495361330479)
XLA Ops:
  0.0 0.0 copy-start.2
  0.0 0.5 %collective-permute-start.1 = (bf16[4096,128]{1,0:T(8,128)(2,1)}, bf16[4096,128]{1,0:T(8,128)(2,1)S(1)}, u32[]{:S(2)}, u32[]{:S(2)}) collective-permute-start(bf16[4096,128]{1,0:T(8,128)(2,1)} %own_hbm.3), channel_id=1, source_target_pairs={{0,1},{1,0},{2,3},{3,2},{4,5},{5,4},{6,7},{7,6},{8,9},{9,8},{10,11... | collective-permute-start | bytes 3145736 | tf_op jit(solution)/shard_map/ppermute | solution.py:81
  0.5 0.3 copy-done.2
  0.8 0.8 %select_bitcast_fusion = (s32[64,128]{1,0:T(8,128)S(1)}, pred[128,64]{0,1:T(8,128)(4,1)S(1)}) fusion(s32[128,64]{0,1:T(8,128)S(1)} %copy-done.2, s32[]{:T(128)S(6)} %mul.23, s32[]{:T(128)S(6)} %mul.22, s32[128,64]{0,1:T(8,128)} %param.5), kind=kLoop, calls=%fused_computation.2 | loop fusion | flops 65536 | bytes 106504 | tf_op jit(solution)/shard_map/transpose | solution.py:93
  1.6 3.1 %collective-permute-start = (s32[64,128]{1,0:T(8,128)S(1)}, s32[64,128]{1,0:T(8,128)S(1)}, u32[]{:S(2)}, u32[]{:S(2)}) collective-permute-start(s32[64,128]{1,0:T(8,128)S(1)} %select_bitcast_fusion.1), channel_id=1, source_target_pairs={{0,2},{1,3},{2,0},{3,1},{4,6},{5,7},{6,4},{7,5},{8,10},{9,11},{10,... | collective-permute-start | bytes 98312 | tf_op jit(solution)/shard_map/ppermute | solution.py:81
  4.6 0.0 collective-permute-done.1.other_ref
  4.6 0.0 copy-start
  4.6 1.2 %copy-done = bf16[4096,128]{1,0:T(8,128)(2,1)S(1)} copy-done((bf16[4096,128]{1,0:T(8,128)(2,1)S(1)}, bf16[4096,128]{1,0:T(8,128)(2,1)}, u32[]{:S(2)}) %copy-start) | copy-done | bytes 1048600
  5.9 0.0 copy-start.1
  5.9 2.1 %shard_map.37 = f32[128,128]{1,0:T(8,128)S(1)} custom-call(s32[64,128]{1,0:T(8,128)S(1)} %get-tuple-element.11.key_ref, bf16[4096,128]{1,0:T(8,128)(2,1)S(1)} %copy-done, bf16[4096,128]{1,0:T(8,128)(2,1)S(1)} %collective-permute-done.1.other_ref), custom_call_target="tpu_custom_call" | custom-call | flops 536870912 | bytes 2097152 | tf_op jit(solution)/shard_map/pallas_call | solution.py:61
  8.0 0.0 collective-permute-done.key_ref
  8.0 0.0 copy-done.1
  8.0 2.1 %shard_map.38 = f32[128,128]{1,0:T(8,128)S(1)} custom-call(s32[64,128]{1,0:T(8,128)S(1)} %collective-permute-done.key_ref, bf16[4096,128]{1,0:T(8,128)(2,1)S(1)} %copy-done.1, bf16[4096,128]{1,0:T(8,128)(2,1)S(1)} %collective-permute-done.1.other_ref), custom_call_target="tpu_custom_call" | custom-call | flops 536870912 | bytes 2097152 | tf_op jit(solution)/shard_map/pallas_call | solution.py:61
  10.2 1.3 %collective-permute-start.2 = (f32[128,128]{1,0:T(8,128)S(1)}, f32[128,128]{1,0:T(8,128)S(1)}, u32[]{:S(2)}, u32[]{:S(2)}) collective-permute-start(f32[128,128]{1,0:T(8,128)S(1)} %shard_map.38), channel_id=1, source_target_pairs={{0,2},{1,3},{2,0},{3,1},{4,6},{5,7},{6,4},{7,5},{8,10},{9,11},{10,... | collective-permute-start | bytes 196616 | tf_op jit(solution)/shard_map/ppermute | solution.py:81
  11.5 3.0 %collective-permute-done.2 = f32[128,128]{1,0:T(8,128)S(1)} collective-permute-done((f32[128,128]{1,0:T(8,128)S(1)}, f32[128,128]{1,0:T(8,128)S(1)}, u32[]{:S(2)}, u32[]{:S(2)}) %collective-permute-start.2) | collective-permute-done | bytes 65568 | tf_op jit(solution)/shard_map/ppermute | solution.py:81
  14.5 1.6 %collective-permute-start.3 = (f32[128,128]{1,0:T(8,128)S(1)}, f32[128,128]{1,0:T(8,128)S(1)}, u32[]{:S(2)}, u32[]{:S(2)}) collective-permute-start(f32[128,128]{1,0:T(8,128)S(1)} %add.31), channel_id=1, source_target_pairs={{0,4},{4,0},{8,12},{12,8},{16,20},{20,16},{24,28},{28,24},{1,5},{5... | collective-permute-start | bytes 196616 | tf_op jit(solution)/shard_map/ppermute | solution.py:81
  16.1 2.8 %collective-permute-done.3 = f32[128,128]{1,0:T(8,128)S(1)} collective-permute-done((f32[128,128]{1,0:T(8,128)S(1)}, f32[128,128]{1,0:T(8,128)S(1)}, u32[]{:S(2)}, u32[]{:S(2)}) %collective-permute-start.3) | collective-permute-done | bytes 65568 | tf_op jit(solution)/shard_map/ppermute | solution.py:81
  18.9 1.6 %collective-permute-start.4 = (f32[128,128]{1,0:T(8,128)S(1)}, f32[128,128]{1,0:T(8,128)S(1)}, u32[]{:S(2)}, u32[]{:S(2)}) collective-permute-start(f32[128,128]{1,0:T(8,128)S(1)} %add.32), channel_id=1, source_target_pairs={{0,8},{4,12},{8,0},{12,4},{16,24},{20,28},{24,16},{28,20},{1,9},{5... | collective-permute-start | bytes 196616 | tf_op jit(solution)/shard_map/ppermute | solution.py:81
  20.5 2.7 %collective-permute-done.4 = f32[128,128]{1,0:T(8,128)S(1)} collective-permute-done((f32[128,128]{1,0:T(8,128)S(1)}, f32[128,128]{1,0:T(8,128)S(1)}, u32[]{:S(2)}, u32[]{:S(2)}) %collective-permute-start.4) | collective-permute-done | bytes 65568 | tf_op jit(solution)/shard_map/ppermute | solution.py:81
  23.2 3.0 %collective-permute-start.5 = (f32[128,128]{1,0:T(8,128)S(1)}, f32[128,128]{1,0:T(8,128)S(1)}, u32[]{:S(2)}, u32[]{:S(2)}) collective-permute-start(f32[128,128]{1,0:T(8,128)S(1)} %add.33), channel_id=1, source_target_pairs={{0,16},{4,20},{8,24},{12,28},{16,0},{20,4},{24,8},{28,12},{1,17},{... | collective-permute-start | bytes 196616 | tf_op jit(solution)/shard_map/ppermute | solution.py:81
  26.2 2.2 %collective-permute-done.5 = f32[128,128]{1,0:T(8,128)S(1)} collective-permute-done((f32[128,128]{1,0:T(8,128)S(1)}, f32[128,128]{1,0:T(8,128)S(1)}, u32[]{:S(2)}, u32[]{:S(2)}) %collective-permute-start.5) | collective-permute-done | bytes 65568 | tf_op jit(solution)/shard_map/ppermute | solution.py:81
  28.5 0.1 multiply_reduce_fusion
  28.6 0.7 %broadcast_divide_fusion = f32[128,128]{1,0:T(8,128)} fusion(f32[128,128]{1,0:T(8,128)S(1)} %get-tuple-element.10, f32[128]{0:T(128)S(1)} %add_sqrt_fusion), kind=kLoop, calls=%fused_computation.1 | loop fusion | flops 16384 | bytes 131584 | tf_op jit(solution)/shard_map/div | solution.py:107
  (5 shorter events, 0.1 us)
Async XLA Ops:
  0.0 0.8 %copy-start.2 = (s32[128,64]{0,1:T(8,128)S(1)}, s32[128,64]{0,1:T(8,128)}, u32[]{:S(2)}) copy-start(s32[128,64]{0,1:T(8,128)} %param.4) | copy-start | bytes 98308
  0.0 4.6 %collective-permute-start.1 = (bf16[4096,128]{1,0:T(8,128)(2,1)}, bf16[4096,128]{1,0:T(8,128)(2,1)S(1)}, u32[]{:S(2)}, u32[]{:S(2)}) collective-permute-start(bf16[4096,128]{1,0:T(8,128)(2,1)} %own_hbm.3), channel_id=1, source_target_pairs={{0,1},{1,0},{2,3},{3,2},{4,5},{5,4},{6,7},{7,6},{8,9},{9,8},{10,11... | collective-permute-start | bytes 3145736 | tf_op jit(solution)/shard_map/ppermute | solution.py:81
  1.6 6.4 %collective-permute-start = (s32[64,128]{1,0:T(8,128)S(1)}, s32[64,128]{1,0:T(8,128)S(1)}, u32[]{:S(2)}, u32[]{:S(2)}) collective-permute-start(s32[64,128]{1,0:T(8,128)S(1)} %select_bitcast_fusion.1), channel_id=1, source_target_pairs={{0,2},{1,3},{2,0},{3,1},{4,6},{5,7},{6,4},{7,5},{8,10},{9,11},{10,... | collective-permute-start | bytes 98312 | tf_op jit(solution)/shard_map/ppermute | solution.py:81
  4.6 1.2 %copy-start = (bf16[4096,128]{1,0:T(8,128)(2,1)S(1)}, bf16[4096,128]{1,0:T(8,128)(2,1)}, u32[]{:S(2)}) copy-start(bf16[4096,128]{1,0:T(8,128)(2,1)} %own_hbm.3) | copy-start | bytes 3145732
  5.9 2.2 %copy-start.1 = (bf16[4096,128]{1,0:T(8,128)(2,1)S(1)}, bf16[4096,128]{1,0:T(8,128)(2,1)}, u32[]{:S(2)}) copy-start(bf16[4096,128]{1,0:T(8,128)(2,1)} %own_hbm.3) | copy-start | bytes 3145732
  10.2 4.3 %collective-permute-start.2 = (f32[128,128]{1,0:T(8,128)S(1)}, f32[128,128]{1,0:T(8,128)S(1)}, u32[]{:S(2)}, u32[]{:S(2)}) collective-permute-start(f32[128,128]{1,0:T(8,128)S(1)} %shard_map.38), channel_id=1, source_target_pairs={{0,2},{1,3},{2,0},{3,1},{4,6},{5,7},{6,4},{7,5},{8,10},{9,11},{10,... | collective-permute-start | bytes 196616 | tf_op jit(solution)/shard_map/ppermute | solution.py:81
  14.5 4.3 %collective-permute-start.3 = (f32[128,128]{1,0:T(8,128)S(1)}, f32[128,128]{1,0:T(8,128)S(1)}, u32[]{:S(2)}, u32[]{:S(2)}) collective-permute-start(f32[128,128]{1,0:T(8,128)S(1)} %add.31), channel_id=1, source_target_pairs={{0,4},{4,0},{8,12},{12,8},{16,20},{20,16},{24,28},{28,24},{1,5},{5... | collective-permute-start | bytes 196616 | tf_op jit(solution)/shard_map/ppermute | solution.py:81
  18.9 4.3 %collective-permute-start.4 = (f32[128,128]{1,0:T(8,128)S(1)}, f32[128,128]{1,0:T(8,128)S(1)}, u32[]{:S(2)}, u32[]{:S(2)}) collective-permute-start(f32[128,128]{1,0:T(8,128)S(1)} %add.32), channel_id=1, source_target_pairs={{0,8},{4,12},{8,0},{12,4},{16,24},{20,28},{24,16},{28,20},{1,9},{5... | collective-permute-start | bytes 196616 | tf_op jit(solution)/shard_map/ppermute | solution.py:81
  23.2 5.3 %collective-permute-start.5 = (f32[128,128]{1,0:T(8,128)S(1)}, f32[128,128]{1,0:T(8,128)S(1)}, u32[]{:S(2)}, u32[]{:S(2)}) collective-permute-start(f32[128,128]{1,0:T(8,128)S(1)} %add.33), channel_id=1, source_target_pairs={{0,16},{4,20},{8,24},{12,28},{16,0},{20,4},{24,8},{28,12},{1,17},{... | collective-permute-start | bytes 196616 | tf_op jit(solution)/shard_map/ppermute | solution.py:81

commit v3 on v2

v3 whole, which is shorter than its diff:
```python
import functools

import jax
import jax.numpy as jnp
from jax import lax
from jax.experimental import pallas as pl
from jax.experimental.pallas import tpu as pltpu
from jax.sharding import PartitionSpec as P

LANES = 128
GAP = 4


def count(key_ref, m_ref, low_ref, cnt_ref, highs):
    length, nbags = key_ref.shape
    per = LANES // length
    prow = nbags // per
    lane = lax.broadcasted_iota(jnp.int32, (prow, LANES), 1)
    odd = lax.broadcasted_iota(jnp.int32, (prow, LANES), 0) & 1
    keys = jnp.concatenate([key_ref[...]] * per, axis=0).T
    local = keys[:prow]
    for j in range(1, per):
        local = jnp.where(lane >= j * length, keys[j * prow : (j + 1) * prow], local)
    row = lax.axis_index("rows")
    half = highs // 2 * LANES
    local = local - (lax.axis_index("rep") * lax.axis_size("rows") + (row & -2)) * half
    inside = (local >= 0) & (local < 2 * half)
    local = local ^ ((row & 1) * half)
    m = lax.shift_right_arithmetic(local, LANES.bit_length() - 1) + highs * (lane // length + per * odd)
    m_ref[...] = jnp.where(inside, m, -1).astype(jnp.float32)
    low_ref[...] = (local & (LANES - 1)).astype(jnp.float32)
    pitch = nbags + GAP
    nums = lax.broadcasted_iota(jnp.int32, (max(2 * per * highs, LANES), LANES), 0)
    nums = nums.astype(jnp.float32).astype(jnp.bfloat16)
    one, zero = jnp.bfloat16(1), jnp.bfloat16(0)

    def hot(row, n):
        row = jnp.broadcast_to(row, (16, LANES)).astype(jnp.bfloat16)
        return jnp.concatenate([jnp.where(nums[k : k + 16] == row, one, zero) for k in range(0, n, 16)], axis=0)

    for p in range(0, prow, 2):
        lhs = jnp.concatenate([hot(m_ref[k : k + 1, :], 2 * per * highs) for k in (p, p + 1)], axis=1)
        rhs = jnp.concatenate([hot(low_ref[k : k + 1, :], LANES) for k in (p, p + 1)], axis=1)
        cnt = lax.dot_general(lhs, rhs, (((1,), (1,)), ((), ())), preferred_element_type=jnp.float32)
        for i in range(2 * per):
            bag = (i % per) * prow + p + i // per
            for h in range(0, highs, 8):
                cnt_ref[pl.ds(h * pitch + bag, 8, stride=pitch), :] = cnt[i * highs + h : i * highs + h + 8, :]


def product(cnt_ref, own_ref, other_ref, out_ref, highs):
    nbags = out_ref.shape[0]
    pitch = nbags + GAP
    acc = jnp.zeros(out_ref.shape, jnp.float32)
    for h in range(0, highs, 2):
        counts = [cnt_ref[k * pitch : k * pitch + nbags, :].astype(jnp.bfloat16) for k in (h, h + 1)]
        table, at = (own_ref, h) if 2 * h < highs else (other_ref, h - highs // 2)
        rows = table[at * LANES : (at + 2) * LANES, :]
        acc += jnp.dot(jnp.concatenate(counts, axis=1), rows, preferred_element_type=jnp.float32)
    out_ref[...] = acc


def count_kernel(key_ref, cnt_ref, m_ref, low_ref, *, highs):
    count(key_ref, m_ref, low_ref, cnt_ref, highs)


def product_kernel(cnt_ref, own_ref, other_ref, out_ref, *, highs):
    product(cnt_ref, own_ref, other_ref, out_ref, highs)


def pool_kernel(key_ref, own_ref, other_ref, out_ref, m_ref, low_ref, cnt_ref, *, highs):
    count(key_ref, m_ref, low_ref, cnt_ref, highs)
    product(cnt_ref, own_ref, other_ref, out_ref, highs)


def pool(key, own, other, split):
    (length, nbags), (rows, width) = key.shape, own.shape
    highs = 2 * rows // LANES
    packed = pltpu.VMEM((nbags * length // LANES, LANES), jnp.float32)
    counts = (highs * (nbags + GAP), LANES)

    def call(kernel, operands, out, scratch, flops):
        return pl.pallas_call(
            functools.partial(kernel, highs=highs),
            out_shape=jax.ShapeDtypeStruct(out, jnp.float32),
            in_specs=[pl.BlockSpec(memory_space=pltpu.VMEM)] * len(operands),
            out_specs=pl.BlockSpec(memory_space=pltpu.VMEM),
            scratch_shapes=scratch,
            cost_estimate=pl.CostEstimate(flops=flops, bytes_accessed=0, transcendentals=0),
            compiler_params=pltpu.CompilerParams(vmem_limit_bytes=16 << 20),
        )(*operands)

    flops = 4 * nbags * rows * width
    if split:
        cnt = call(count_kernel, (key,), counts, [packed, packed], 2 * flops)
        return call(product_kernel, (cnt, own, other), (nbags, width), [], flops)
    scratch = [packed, packed, pltpu.VMEM(counts, jnp.float32)]
    return call(pool_kernel, (key, own, other), (nbags, width), scratch, 3 * flops)


def swap(value, axis, size, bit):
    return lax.ppermute(value, axis, [(i, i ^ bit) for i in range(size)])


def on_device(rows_size, rep_size, item_table, history_ids, history_mask):
    other = swap(item_table, "rows", rows_size, 1)
    key = jnp.where(history_mask > 0, history_ids, -1).T
    keys = [swap(key, "rows", rows_size, s) for s in range(2, rows_size, 2)]
    near = pool(key, item_table, other, True)
    keys, near = lax.optimization_barrier((keys, near))
    def hop(value, row_bit, rep_bit):
        both = rep_bit * rows_size + row_bit
        return lax.ppermute(value, ("rep", "rows"), [(i, i ^ both) for i in range(rows_size * rep_size)])

    sums = [near] + [pool(k, item_table, other, False) for k in keys]
    while len(sums) > 2:
        half = len(sums) // 2
        sums = [a + swap(b, "rows", rows_size, 2 * half) for a, b in zip(sums[:half], sums[half:])]
    near, far = sums
    pooled = near + hop(near, 0, 1) + (hop(far, 2, 0) + hop(far, 2, 1))
    bit = 2
    while 2 * bit < rep_size:
        pooled = pooled + hop(pooled, 0, 1 * bit) + (hop(pooled, 0, 3 * bit) + hop(pooled, 0, 2 * bit))
        bit *= 4
    while bit < rep_size:
        pooled = pooled + hop(pooled, 0, bit)
        bit *= 2
    return pooled / jnp.sqrt(jnp.mean(pooled * pooled, axis=1, keepdims=True) + 1e-06)


def solution(mesh):
    body = functools.partial(on_device, mesh.shape["rows"], mesh.shape["rep"])
    return jax.shard_map(
        body,
        mesh=mesh,
        in_specs=(P(("rep", "rows"), None), P("rows", None), P("rows", None)),
        out_specs=P("rows", None),
        check_vma=False,
    )
```

time: 29.6 us -> 25.6 us (0.86)
  waiting for transfers between devices: 10.8 us -> 8.78 us
  local copies, waits for them, and re-layouts: 1.49 us -> 0.01 us
    ppermute x6 -> x2, waiting for transfers between devices: 10.8 us -> 0.01 us  [swap(): return lax.ppermute(value, axis, [(i, i ^ bit) for i in range(size)])]
    ppermute x0 -> x6, waiting for transfers between devices: none -> 8.78 us  [hop(): lax.ppermute(value, ('rep', 'rows'), [(i, i ^ both) for i in range(rows_s...]
    ppermute x6 -> x2, starting transfers between devices: 11.1 us -> 3.09 us  [swap(): return lax.ppermute(value, axis, [(i, i ^ bit) for i in range(size)])]
    ppermute x0 -> x6, starting transfers between devices: none -> 7.78 us  [hop(): lax.ppermute(value, ('rep', 'rows'), [(i, i ^ both) for i in range(rows_s...]
    unnamed x6 -> x2, local copies, waits for them, and re-layouts: 1.49 us -> 0.01 us
    pallas_call x2 -> x3, Pallas kernels: 4.28 us -> 4.06 us  [call(): pl.pallas_call(functools.partial(kernel, highs=highs), out_shape=jax.Shap...]
    transpose x2 -> x1, other arithmetic: 0.8 us -> 0.78 us  [on_device(): key = jnp.where(history_mask > 0, history_ids, -1).T]
  transfers between devices with their start and end apart: 6 -> 8, of which waited for: 4 -> 6; matrix products, arithmetic and copies ran while one was open for 3% -> 3% of each run, Pallas kernels for 7% -> 8%
where the time goes in v3:
time: 25.6 us; the launch traced here: 25.4 us
  starting transfers between devices  10.9 us (43%)
  waiting for transfers between devices  8.78 us (34%)
  Pallas kernels  4.06 us (16%)
  other arithmetic  1.64 us (6%)
    ppermute x6, waiting for transfers between devices, hop(): lax.ppermute(value, ('rep', 'rows'), [(i, i ^ both) for i in range(rows_s...  8.78 us
    ppermute x6, starting transfers between devices, hop(): lax.ppermute(value, ('rep', 'rows'), [(i, i ^ both) for i in range(rows_s...  7.78 us
    pallas_call x3, Pallas kernels, call(): pl.pallas_call(functools.partial(kernel, highs=highs), out_shape=jax.Shap...  4.06 us
    ppermute x2, starting transfers between devices, swap(): return lax.ppermute(value, axis, [(i, i ^ bit) for i in range(size)])  3.09 us
    transpose x1, other arithmetic, on_device(): key = jnp.where(history_mask > 0, history_ids, -1).T  0.78 us
    div x1, other arithmetic, on_device(): pooled / jnp.sqrt(jnp.mean(pooled * pooled, axis=1, keepdims=True) + 1e-06)  0.73 us
  transfers between devices with their start and end apart: 8, of which 6 were waited for; matrix products, arithmetic and copies ran while one was open for 3% of the time, Pallas kernels for 8%

profile of v3, /device:TPU:0, one launch (start us, length us, event | category | flops | bytes accessed | tf_op | source)
XLA Modules:
  0.0 25.4 jit_solution(16677865167968942250)
XLA Ops:
  0.0 0.0 copy-start
  0.0 0.5 %collective-permute-start.1 = (bf16[4096,128]{1,0:T(8,128)(2,1)}, bf16[4096,128]{1,0:T(8,128)(2,1)S(1)}, u32[]{:S(2)}, u32[]{:S(2)}) collective-permute-start(bf16[4096,128]{1,0:T(8,128)(2,1)} %own_ref.3), channel_id=1, source_target_pairs={{0,1},{1,0},{2,3},{3,2},{4,5},{5,4},{6,7},{7,6},{8,9},{9,8},{10,11... | collective-permute-start | bytes 3145736 | tf_op jit(solution)/shard_map/ppermute | solution.py:102
  0.5 0.8 %select_bitcast_fusion.key_ref = s32[64,128]{1,0:T(8,128)S(1)} fusion(s32[128,64]{0,1:T(8,128)} %param.4, s32[128,64]{0,1:T(8,128)} %param.5), kind=kLoop, calls=%fused_computation.4 | loop fusion | flops 16384 | bytes 98304 | tf_op jit(solution)/shard_map/transpose | solution.py:107
  1.3 2.6 %collective-permute-start = (s32[64,128]{1,0:T(8,128)S(1)}, s32[64,128]{1,0:T(8,128)S(1)}, u32[]{:S(2)}, u32[]{:S(2)}) collective-permute-start(s32[64,128]{1,0:T(8,128)S(1)} %select_bitcast_fusion.key_ref), channel_id=1, source_target_pairs={{0,2},{1,3},{2,0},{3,1},{4,6},{5,7},{6,4},{7,5},{8,10},{9,11},{10,... | collective-permute-start | bytes 98312 | tf_op jit(solution)/shard_map/ppermute | solution.py:102
  3.9 1.4 %shard_map.37.cnt_ref = f32[8448,128]{1,0:T(8,128)S(1)} custom-call(s32[64,128]{1,0:T(8,128)S(1)} %select_bitcast_fusion.key_ref), custom_call_target="tpu_custom_call" | custom-call | flops 536870912 | tf_op jit(solution)/shard_map/pallas_call | solution.py:83
  5.2 0.0 collective-permute-done.1.other_ref
  5.2 0.0 copy-done
  5.3 0.7 %shard_map.38 = f32[128,128]{1,0:T(8,128)S(1)} custom-call(f32[8448,128]{1,0:T(8,128)S(1)} %shard_map.37.cnt_ref, bf16[4096,128]{1,0:T(8,128)(2,1)S(1)} %copy-done, bf16[4096,128]{1,0:T(8,128)(2,1)S(1)} %collective-permute-done.1.other_ref), custom_call_target="tpu_custom_call" | custom-call | flops 268435456 | tf_op jit(solution)/shard_map/pallas_call | solution.py:83
  6.0 0.0 collective-permute-done.key_ref
  6.0 2.0 %shard_map.39 = f32[128,128]{1,0:T(8,128)S(1)} custom-call(s32[64,128]{1,0:T(8,128)S(1)} %collective-permute-done.key_ref, bf16[4096,128]{1,0:T(8,128)(2,1)S(1)} %copy-done, bf16[4096,128]{1,0:T(8,128)(2,1)S(1)} %collective-permute-done.1.other_ref), custom_call_target="tpu_custom_call" | custom-call | flops 805306368 | tf_op jit(solution)/shard_map/pallas_call | solution.py:83
  8.0 2.8 %collective-permute-start.4 = (f32[128,128]{1,0:T(8,128)S(1)}, f32[128,128]{1,0:T(8,128)S(1)}, u32[]{:S(2)}, u32[]{:S(2)}) collective-permute-start(f32[128,128]{1,0:T(8,128)S(1)} %shard_map.39), channel_id=1, source_target_pairs={{0,6},{1,7},{2,4},{3,5},{4,2},{5,3},{6,0},{7,1},{8,14},{9,15},{10,... | collective-permute-start | bytes 196616 | tf_op jit(solution)/shard_map/ppermute | solution.py:113
  10.8 0.5 %collective-permute-start.3 = (f32[128,128]{1,0:T(8,128)S(1)}, f32[128,128]{1,0:T(8,128)S(1)}, u32[]{:S(2)}, u32[]{:S(2)}) collective-permute-start(f32[128,128]{1,0:T(8,128)S(1)} %shard_map.39), channel_id=1, source_target_pairs={{0,2},{1,3},{2,0},{3,1},{4,6},{5,7},{6,4},{7,5},{8,10},{9,11},{10,... | collective-permute-start | bytes 196616 | tf_op jit(solution)/shard_map/ppermute | solution.py:113
  11.3 0.2 collective-permute-start.2
  11.5 1.8 %collective-permute-done.4 = f32[128,128]{1,0:T(8,128)S(1)} collective-permute-done((f32[128,128]{1,0:T(8,128)S(1)}, f32[128,128]{1,0:T(8,128)S(1)}, u32[]{:S(2)}, u32[]{:S(2)}) %collective-permute-start.4) | collective-permute-done | bytes 65568 | tf_op jit(solution)/shard_map/ppermute | solution.py:113
  13.3 1.8 %collective-permute-done.3 = f32[128,128]{1,0:T(8,128)S(1)} collective-permute-done((f32[128,128]{1,0:T(8,128)S(1)}, f32[128,128]{1,0:T(8,128)S(1)}, u32[]{:S(2)}, u32[]{:S(2)}) %collective-permute-start.3) | collective-permute-done | bytes 65568 | tf_op jit(solution)/shard_map/ppermute | solution.py:113
  15.1 0.5 %collective-permute-done.2 = f32[128,128]{1,0:T(8,128)S(1)} collective-permute-done((f32[128,128]{1,0:T(8,128)S(1)}, f32[128,128]{1,0:T(8,128)S(1)}, u32[]{:S(2)}, u32[]{:S(2)}) %collective-permute-start.2) | collective-permute-done | bytes 65568 | tf_op jit(solution)/shard_map/ppermute | solution.py:113
  15.6 2.6 %collective-permute-start.7 = (f32[128,128]{1,0:T(8,128)S(1)}, f32[128,128]{1,0:T(8,128)S(1)}, u32[]{:S(2)}, u32[]{:S(2)}) collective-permute-start(f32[128,128]{1,0:T(8,128)S(1)} %add_add_fusion.1), channel_id=1, source_target_pairs={{0,16},{1,17},{2,18},{3,19},{4,20},{5,21},{6,22},{7,23},{8,24},{9,... | collective-permute-start | bytes 196616 | tf_op jit(solution)/shard_map/ppermute | solution.py:113
  18.2 1.3 %collective-permute-start.6 = (f32[128,128]{1,0:T(8,128)S(1)}, f32[128,128]{1,0:T(8,128)S(1)}, u32[]{:S(2)}, u32[]{:S(2)}) collective-permute-start(f32[128,128]{1,0:T(8,128)S(1)} %add_add_fusion.1), channel_id=1, source_target_pairs={{0,24},{1,25},{2,26},{3,27},{4,28},{5,29},{6,30},{7,31},{8,16},{9,... | collective-permute-start | bytes 196616 | tf_op jit(solution)/shard_map/ppermute | solution.py:113
  19.6 0.2 collective-permute-start.5
  19.8 3.1 %collective-permute-done.7 = f32[128,128]{1,0:T(8,128)S(1)} collective-permute-done((f32[128,128]{1,0:T(8,128)S(1)}, f32[128,128]{1,0:T(8,128)S(1)}, u32[]{:S(2)}, u32[]{:S(2)}) %collective-permute-start.7) | collective-permute-done | bytes 65568 | tf_op jit(solution)/shard_map/ppermute | solution.py:113
  22.9 1.5 %collective-permute-done.6 = f32[128,128]{1,0:T(8,128)S(1)} collective-permute-done((f32[128,128]{1,0:T(8,128)S(1)}, f32[128,128]{1,0:T(8,128)S(1)}, u32[]{:S(2)}, u32[]{:S(2)}) %collective-permute-start.6) | collective-permute-done | bytes 65568 | tf_op jit(solution)/shard_map/ppermute | solution.py:113
  24.4 0.2 collective-permute-done.5
  24.6 0.1 multiply_reduce_fusion
  24.7 0.7 %broadcast_divide_fusion = f32[128,128]{1,0:T(8,128)} fusion(f32[128,128]{1,0:T(8,128)S(1)} %get-tuple-element.10, f32[128]{0:T(128)S(1)} %add_sqrt_fusion), kind=kLoop, calls=%fused_computation.3 | loop fusion | flops 16384 | bytes 131584 | tf_op jit(solution)/shard_map/div | solution.py:128
  (2 shorter events, 0.0 us)
Async XLA Ops:
  0.0 5.2 %copy-start = (bf16[4096,128]{1,0:T(8,128)(2,1)S(1)}, bf16[4096,128]{1,0:T(8,128)(2,1)}, u32[]{:S(2)}) copy-start(bf16[4096,128]{1,0:T(8,128)(2,1)} %own_ref.3) | copy-start | bytes 3145732
  0.0 5.2 %collective-permute-start.1 = (bf16[4096,128]{1,0:T(8,128)(2,1)}, bf16[4096,128]{1,0:T(8,128)(2,1)S(1)}, u32[]{:S(2)}, u32[]{:S(2)}) collective-permute-start(bf16[4096,128]{1,0:T(8,128)(2,1)} %own_ref.3), channel_id=1, source_target_pairs={{0,1},{1,0},{2,3},{3,2},{4,5},{5,4},{6,7},{7,6},{8,9},{9,8},{10,11... | collective-permute-start | bytes 3145736 | tf_op jit(solution)/shard_map/ppermute | solution.py:102
  1.3 4.7 %collective-permute-start = (s32[64,128]{1,0:T(8,128)S(1)}, s32[64,128]{1,0:T(8,128)S(1)}, u32[]{:S(2)}, u32[]{:S(2)}) collective-permute-start(s32[64,128]{1,0:T(8,128)S(1)} %select_bitcast_fusion.key_ref), channel_id=1, source_target_pairs={{0,2},{1,3},{2,0},{3,1},{4,6},{5,7},{6,4},{7,5},{8,10},{9,11},{10,... | collective-permute-start | bytes 98312 | tf_op jit(solution)/shard_map/ppermute | solution.py:102
  8.0 5.3 %collective-permute-start.4 = (f32[128,128]{1,0:T(8,128)S(1)}, f32[128,128]{1,0:T(8,128)S(1)}, u32[]{:S(2)}, u32[]{:S(2)}) collective-permute-start(f32[128,128]{1,0:T(8,128)S(1)} %shard_map.39), channel_id=1, source_target_pairs={{0,6},{1,7},{2,4},{3,5},{4,2},{5,3},{6,0},{7,1},{8,14},{9,15},{10,... | collective-permute-start | bytes 196616 | tf_op jit(solution)/shard_map/ppermute | solution.py:113
  10.8 4.3 %collective-permute-start.3 = (f32[128,128]{1,0:T(8,128)S(1)}, f32[128,128]{1,0:T(8,128)S(1)}, u32[]{:S(2)}, u32[]{:S(2)}) collective-permute-start(f32[128,128]{1,0:T(8,128)S(1)} %shard_map.39), channel_id=1, source_target_pairs={{0,2},{1,3},{2,0},{3,1},{4,6},{5,7},{6,4},{7,5},{8,10},{9,11},{10,... | collective-permute-start | bytes 196616 | tf_op jit(solution)/shard_map/ppermute | solution.py:113
  11.3 4.3 %collective-permute-start.2 = (f32[128,128]{1,0:T(8,128)S(1)}, f32[128,128]{1,0:T(8,128)S(1)}, u32[]{:S(2)}, u32[]{:S(2)}) collective-permute-start(f32[128,128]{1,0:T(8,128)S(1)} %shard_map.38), channel_id=1, source_target_pairs={{0,4},{1,5},{2,6},{3,7},{4,0},{5,1},{6,2},{7,3},{8,12},{9,13},{10,... | collective-permute-start | bytes 196616 | tf_op jit(solution)/shard_map/ppermute | solution.py:113
  15.6 7.3 %collective-permute-start.7 = (f32[128,128]{1,0:T(8,128)S(1)}, f32[128,128]{1,0:T(8,128)S(1)}, u32[]{:S(2)}, u32[]{:S(2)}) collective-permute-start(f32[128,128]{1,0:T(8,128)S(1)} %add_add_fusion.1), channel_id=1, source_target_pairs={{0,16},{1,17},{2,18},{3,19},{4,20},{5,21},{6,22},{7,23},{8,24},{9,... | collective-permute-start | bytes 196616 | tf_op jit(solution)/shard_map/ppermute | solution.py:113
  18.2 6.2 %collective-permute-start.6 = (f32[128,128]{1,0:T(8,128)S(1)}, f32[128,128]{1,0:T(8,128)S(1)}, u32[]{:S(2)}, u32[]{:S(2)}) collective-permute-start(f32[128,128]{1,0:T(8,128)S(1)} %add_add_fusion.1), channel_id=1, source_target_pairs={{0,24},{1,25},{2,26},{3,27},{4,28},{5,29},{6,30},{7,31},{8,16},{9,... | collective-permute-start | bytes 196616 | tf_op jit(solution)/shard_map/ppermute | solution.py:113
  19.6 5.0 %collective-permute-start.5 = (f32[128,128]{1,0:T(8,128)S(1)}, f32[128,128]{1,0:T(8,128)S(1)}, u32[]{:S(2)}, u32[]{:S(2)}) collective-permute-start(f32[128,128]{1,0:T(8,128)S(1)} %add_add_fusion.1), channel_id=1, source_target_pairs={{0,8},{1,9},{2,10},{3,11},{4,12},{5,13},{6,14},{7,15},{8,0},{9,1},... | collective-permute-start | bytes 196616 | tf_op jit(solution)/shard_map/ppermute | solution.py:113

commit v4 on v3

--- a/solution.py
+++ b/solution.py
@@ -6,6 +6,7 @@
 from jax.experimental import pallas as pl
 from jax.experimental.pallas import tpu as pltpu
 from jax.sharding import PartitionSpec as P
+
 
 LANES = 128
 GAP = 4
@@ -36,7 +37,8 @@
 
     def hot(row, n):
         row = jnp.broadcast_to(row, (16, LANES)).astype(jnp.bfloat16)
-        return jnp.concatenate([jnp.where(nums[k : k + 16] == row, one, zero) for k in range(0, n, 16)], axis=0)
+        tiles = [jnp.where(nums[k : k + 16] == row, one, zero) for k in range(0, n, 16)]
+        return jnp.concatenate(tiles, axis=0).astype(jnp.float8_e4m3fn)
 
     for p in range(0, prow, 2):
         lhs = jnp.concatenate([hot(m_ref[k : k + 1, :], 2 * per * highs) for k in (p, p + 1)], axis=1)
@@ -105,26 +107,34 @@
 def on_device(rows_size, rep_size, item_table, history_ids, history_mask):
     other = swap(item_table, "rows", rows_size, 1)
     key = jnp.where(history_mask > 0, history_ids, -1).T
-    keys = [swap(key, "rows", rows_size, s) for s in range(2, rows_size, 2)]
-    near = pool(key, item_table, other, True)
-    keys, near = lax.optimization_barrier((keys, near))
+
     def hop(value, row_bit, rep_bit):
         both = rep_bit * rows_size + row_bit
         return lax.ppermute(value, ("rep", "rows"), [(i, i ^ both) for i in range(rows_size * rep_size)])
 
-    sums = [near] + [pool(k, item_table, other, False) for k in keys]
+    keys = []
+    for s in range(2, rows_size, 2):
+        keys.append(swap(key, "rows", rows_size, s))
+    near = pool(key, item_table, other, True)
+    sums = []
+    for s, k in zip(range(2, rows_size, 2), keys):
+        sums.append(pool(k, item_table, other, False))
+    sums = [near] + sums
     while len(sums) > 2:
         half = len(sums) // 2
         sums = [a + swap(b, "rows", rows_size, 2 * half) for a, b in zip(sums[:half], sums[half:])]
     near, far = sums
-    pooled = near + hop(near, 0, 1) + (hop(far, 2, 0) + hop(far, 2, 1))
+    across = hop(near, 0, 1)
+    straight = hop(far, 2, 0)
+    crossed = hop(far, 2, 1)
+    pooled = near + across + (straight + crossed)
     bit = 2
-    while 2 * bit < rep_size:
-        pooled = pooled + hop(pooled, 0, 1 * bit) + (hop(pooled, 0, 3 * bit) + hop(pooled, 0, 2 * bit))
+    while bit < rep_size:
+        parts = []
+        for k in (1, 2, 3) if 2 * bit < rep_size else (1,):
+            parts.append(hop(pooled, 0, k * bit))
+        pooled = pooled + sum(parts[1:], parts[0])
         bit *= 4
-    while bit < rep_size:
-        pooled = pooled + hop(pooled, 0, bit)
-        bit *= 2
     return pooled / jnp.sqrt(jnp.mean(pooled * pooled, axis=1, keepdims=True) + 1e-06)
 
 

time: 25.6 us -> 26.3 us (1.027)
  waiting for transfers between devices: 8.78 us -> 9.92 us
  Pallas kernels: 4.06 us -> 3.12 us
  starting transfers between devices: 10.9 us -> 11.4 us
    ppermute x6, waiting for transfers between devices: 8.78 us -> 9.92 us  [hop(): lax.ppermute(value, ('rep', 'rows'), [(i, i ^ both) for i in range(rows_s...]
    pallas_call x3, Pallas kernels: 4.06 us -> 3.12 us  [call(): pl.pallas_call(functools.partial(kernel, highs=highs), out_shape=jax.Shap...]
    ppermute x6, starting transfers between devices: 7.78 us -> 8.28 us  [hop(): lax.ppermute(value, ('rep', 'rows'), [(i, i ^ both) for i in range(rows_s...]
  transfers between devices with their start and end apart: 8 -> 8, of which waited for: 6 -> 5; matrix products, arithmetic and copies ran while one was open for 3% -> 3% of each run, Pallas kernels for 8% -> 12%
where the time goes in v4:
time: 26.3 us; the launch traced here: 26.1 us
  starting transfers between devices  11.4 us (43%)
  waiting for transfers between devices  9.92 us (38%)
  Pallas kernels  3.12 us (12%)
  other arithmetic  1.64 us (6%)
    ppermute x6, waiting for transfers between devices, hop(): lax.ppermute(value, ('rep', 'rows'), [(i, i ^ both) for i in range(rows_s...  9.92 us
    ppermute x6, starting transfers between devices, hop(): lax.ppermute(value, ('rep', 'rows'), [(i, i ^ both) for i in range(rows_s...  8.28 us
    pallas_call x3, Pallas kernels, call(): pl.pallas_call(functools.partial(kernel, highs=highs), out_shape=jax.Shap...  3.12 us
    ppermute x2, starting transfers between devices, swap(): return lax.ppermute(value, axis, [(i, i ^ bit) for i in range(size)])  3.09 us
    transpose x1, other arithmetic, on_device(): key = jnp.where(history_mask > 0, history_ids, -1).T  0.78 us
    div x1, other arithmetic, on_device(): pooled / jnp.sqrt(jnp.mean(pooled * pooled, axis=1, keepdims=True) + 1e-06)  0.73 us
  transfers between devices with their start and end apart: 8, of which 5 were waited for; matrix products, arithmetic and copies ran while one was open for 3% of the time, Pallas kernels for 12%

profile of v4, /device:TPU:0, one launch (start us, length us, event | category | flops | bytes accessed | tf_op | source)
XLA Modules:
  0.0 26.1 jit_solution(15060112742615408072)
XLA Ops:
  0.0 0.0 copy-start
  0.0 0.5 %collective-permute-start = (bf16[4096,128]{1,0:T(8,128)(2,1)}, bf16[4096,128]{1,0:T(8,128)(2,1)S(1)}, u32[]{:S(2)}, u32[]{:S(2)}) collective-permute-start(bf16[4096,128]{1,0:T(8,128)(2,1)} %own_ref.3), channel_id=1, source_target_pairs={{0,1},{1,0},{2,3},{3,2},{4,5},{5,4},{6,7},{7,6},{8,9},{9,8},{10,11... | collective-permute-start | bytes 3145736 | tf_op jit(solution)/shard_map/ppermute | solution.py:104
  0.5 0.8 %select_bitcast_fusion.key_ref = s32[64,128]{1,0:T(8,128)S(1)} fusion(s32[128,64]{0,1:T(8,128)} %param.4, s32[128,64]{0,1:T(8,128)} %param.5), kind=kLoop, calls=%fused_computation.4 | loop fusion | flops 16384 | bytes 98304 | tf_op jit(solution)/shard_map/transpose | solution.py:109
  1.3 2.6 %collective-permute-start.2 = (s32[64,128]{1,0:T(8,128)S(1)}, s32[64,128]{1,0:T(8,128)S(1)}, u32[]{:S(2)}, u32[]{:S(2)}) collective-permute-start(s32[64,128]{1,0:T(8,128)S(1)} %select_bitcast_fusion.key_ref), channel_id=1, source_target_pairs={{0,2},{1,3},{2,0},{3,1},{4,6},{5,7},{6,4},{7,5},{8,10},{9,11},{10,... | collective-permute-start | bytes 98312 | tf_op jit(solution)/shard_map/ppermute | solution.py:104
  3.9 0.9 %shard_map.37.cnt_ref = f32[8448,128]{1,0:T(8,128)S(1)} custom-call(s32[64,128]{1,0:T(8,128)S(1)} %select_bitcast_fusion.key_ref), custom_call_target="tpu_custom_call" | custom-call | flops 536870912 | tf_op jit(solution)/shard_map/pallas_call | solution.py:85
  4.7 0.0 collective-permute-done.other_ref
  4.7 0.0 copy-done
  4.8 0.7 %shard_map.38 = f32[128,128]{1,0:T(8,128)S(1)} custom-call(f32[8448,128]{1,0:T(8,128)S(1)} %shard_map.37.cnt_ref, bf16[4096,128]{1,0:T(8,128)(2,1)S(1)} %copy-done, bf16[4096,128]{1,0:T(8,128)(2,1)S(1)} %collective-permute-done.other_ref), custom_call_target="tpu_custom_call" | custom-call | flops 268435456 | tf_op jit(solution)/shard_map/pallas_call | solution.py:85
  5.5 1.6 %collective-permute-start.1 = (f32[128,128]{1,0:T(8,128)S(1)}, f32[128,128]{1,0:T(8,128)S(1)}, u32[]{:S(2)}, u32[]{:S(2)}) collective-permute-start(f32[128,128]{1,0:T(8,128)S(1)} %shard_map.38), channel_id=1, source_target_pairs={{0,4},{1,5},{2,6},{3,7},{4,0},{5,1},{6,2},{7,3},{8,12},{9,13},{10,... | collective-permute-start | bytes 196616 | tf_op jit(solution)/shard_map/ppermute | solution.py:113
  7.0 0.0 collective-permute-done.2.key_ref
  7.0 1.6 %shard_map.39 = f32[128,128]{1,0:T(8,128)S(1)} custom-call(s32[64,128]{1,0:T(8,128)S(1)} %collective-permute-done.2.key_ref, bf16[4096,128]{1,0:T(8,128)(2,1)S(1)} %copy-done, bf16[4096,128]{1,0:T(8,128)(2,1)S(1)} %collective-permute-done.other_ref), custom_call_target="tpu_custom_call" | custom-call | flops 805306368 | tf_op jit(solution)/shard_map/pallas_call | solution.py:85
  8.6 1.2 %collective-permute-start.3 = (f32[128,128]{1,0:T(8,128)S(1)}, f32[128,128]{1,0:T(8,128)S(1)}, u32[]{:S(2)}, u32[]{:S(2)}) collective-permute-start(f32[128,128]{1,0:T(8,128)S(1)} %shard_map.39), channel_id=1, source_target_pairs={{0,2},{1,3},{2,0},{3,1},{4,6},{5,7},{6,4},{7,5},{8,10},{9,11},{10,... | collective-permute-start | bytes 196616 | tf_op jit(solution)/shard_map/ppermute | solution.py:113
  9.8 1.1 %collective-permute-start.4 = (f32[128,128]{1,0:T(8,128)S(1)}, f32[128,128]{1,0:T(8,128)S(1)}, u32[]{:S(2)}, u32[]{:S(2)}) collective-permute-start(f32[128,128]{1,0:T(8,128)S(1)} %shard_map.39), channel_id=1, source_target_pairs={{0,6},{1,7},{2,4},{3,5},{4,2},{5,3},{6,0},{7,1},{8,14},{9,15},{10,... | collective-permute-start | bytes 196616 | tf_op jit(solution)/shard_map/ppermute | solution.py:113
  10.9 0.0 collective-permute-done.1
  10.9 2.1 %collective-permute-done.3 = f32[128,128]{1,0:T(8,128)S(1)} collective-permute-done((f32[128,128]{1,0:T(8,128)S(1)}, f32[128,128]{1,0:T(8,128)S(1)}, u32[]{:S(2)}, u32[]{:S(2)}) %collective-permute-start.3) | collective-permute-done | bytes 65568 | tf_op jit(solution)/shard_map/ppermute | solution.py:113
  12.9 2.0 %collective-permute-done.4 = f32[128,128]{1,0:T(8,128)S(1)} collective-permute-done((f32[128,128]{1,0:T(8,128)S(1)}, f32[128,128]{1,0:T(8,128)S(1)}, u32[]{:S(2)}, u32[]{:S(2)}) %collective-permute-start.4) | collective-permute-done | bytes 65568 | tf_op jit(solution)/shard_map/ppermute | solution.py:113
  15.0 1.6 %collective-permute-start.5 = (f32[128,128]{1,0:T(8,128)S(1)}, f32[128,128]{1,0:T(8,128)S(1)}, u32[]{:S(2)}, u32[]{:S(2)}) collective-permute-start(f32[128,128]{1,0:T(8,128)S(1)} %add_add_fusion.1), channel_id=1, source_target_pairs={{0,8},{1,9},{2,10},{3,11},{4,12},{5,13},{6,14},{7,15},{8,0},{9,1},... | collective-permute-start | bytes 196616 | tf_op jit(solution)/shard_map/ppermute | solution.py:113
  16.6 2.6 %collective-permute-start.6 = (f32[128,128]{1,0:T(8,128)S(1)}, f32[128,128]{1,0:T(8,128)S(1)}, u32[]{:S(2)}, u32[]{:S(2)}) collective-permute-start(f32[128,128]{1,0:T(8,128)S(1)} %add_add_fusion.1), channel_id=1, source_target_pairs={{0,16},{1,17},{2,18},{3,19},{4,20},{5,21},{6,22},{7,23},{8,24},{9,... | collective-permute-start | bytes 196616 | tf_op jit(solution)/shard_map/ppermute | solution.py:113
  19.2 0.2 collective-permute-start.7
  19.4 0.2 collective-permute-done.5
  19.7 3.5 %collective-permute-done.6 = f32[128,128]{1,0:T(8,128)S(1)} collective-permute-done((f32[128,128]{1,0:T(8,128)S(1)}, f32[128,128]{1,0:T(8,128)S(1)}, u32[]{:S(2)}, u32[]{:S(2)}) %collective-permute-start.6) | collective-permute-done | bytes 65568 | tf_op jit(solution)/shard_map/ppermute | solution.py:113
  23.2 2.1 %collective-permute-done.7 = f32[128,128]{1,0:T(8,128)S(1)} collective-permute-done((f32[128,128]{1,0:T(8,128)S(1)}, f32[128,128]{1,0:T(8,128)S(1)}, u32[]{:S(2)}, u32[]{:S(2)}) %collective-permute-start.7) | collective-permute-done | bytes 65568 | tf_op jit(solution)/shard_map/ppermute | solution.py:113
  25.3 0.1 multiply_reduce_fusion
  25.4 0.7 %broadcast_divide_fusion = f32[128,128]{1,0:T(8,128)} fusion(f32[128,128]{1,0:T(8,128)S(1)} %get-tuple-element.6, f32[128]{0:T(128)S(1)} %add_sqrt_fusion), kind=kLoop, calls=%fused_computation.3 | loop fusion | flops 16384 | bytes 131584 | tf_op jit(solution)/shard_map/div | solution.py:138
  (2 shorter events, 0.0 us)
Async XLA Ops:
  0.0 4.7 %copy-start = (bf16[4096,128]{1,0:T(8,128)(2,1)S(1)}, bf16[4096,128]{1,0:T(8,128)(2,1)}, u32[]{:S(2)}) copy-start(bf16[4096,128]{1,0:T(8,128)(2,1)} %own_ref.3) | copy-start | bytes 3145732
  0.0 4.7 %collective-permute-start = (bf16[4096,128]{1,0:T(8,128)(2,1)}, bf16[4096,128]{1,0:T(8,128)(2,1)S(1)}, u32[]{:S(2)}, u32[]{:S(2)}) collective-permute-start(bf16[4096,128]{1,0:T(8,128)(2,1)} %own_ref.3), channel_id=1, source_target_pairs={{0,1},{1,0},{2,3},{3,2},{4,5},{5,4},{6,7},{7,6},{8,9},{9,8},{10,11... | collective-permute-start | bytes 3145736 | tf_op jit(solution)/shard_map/ppermute | solution.py:104
  1.3 5.7 %collective-permute-start.2 = (s32[64,128]{1,0:T(8,128)S(1)}, s32[64,128]{1,0:T(8,128)S(1)}, u32[]{:S(2)}, u32[]{:S(2)}) collective-permute-start(s32[64,128]{1,0:T(8,128)S(1)} %select_bitcast_fusion.key_ref), channel_id=1, source_target_pairs={{0,2},{1,3},{2,0},{3,1},{4,6},{5,7},{6,4},{7,5},{8,10},{9,11},{10,... | collective-permute-start | bytes 98312 | tf_op jit(solution)/shard_map/ppermute | solution.py:104
  5.5 5.4 %collective-permute-start.1 = (f32[128,128]{1,0:T(8,128)S(1)}, f32[128,128]{1,0:T(8,128)S(1)}, u32[]{:S(2)}, u32[]{:S(2)}) collective-permute-start(f32[128,128]{1,0:T(8,128)S(1)} %shard_map.38), channel_id=1, source_target_pairs={{0,4},{1,5},{2,6},{3,7},{4,0},{5,1},{6,2},{7,3},{8,12},{9,13},{10,... | collective-permute-start | bytes 196616 | tf_op jit(solution)/shard_map/ppermute | solution.py:113
  8.6 4.3 %collective-permute-start.3 = (f32[128,128]{1,0:T(8,128)S(1)}, f32[128,128]{1,0:T(8,128)S(1)}, u32[]{:S(2)}, u32[]{:S(2)}) collective-permute-start(f32[128,128]{1,0:T(8,128)S(1)} %shard_map.39), channel_id=1, source_target_pairs={{0,2},{1,3},{2,0},{3,1},{4,6},{5,7},{6,4},{7,5},{8,10},{9,11},{10,... | collective-permute-start | bytes 196616 | tf_op jit(solution)/shard_map/ppermute | solution.py:113
  9.8 5.2 %collective-permute-start.4 = (f32[128,128]{1,0:T(8,128)S(1)}, f32[128,128]{1,0:T(8,128)S(1)}, u32[]{:S(2)}, u32[]{:S(2)}) collective-permute-start(f32[128,128]{1,0:T(8,128)S(1)} %shard_map.39), channel_id=1, source_target_pairs={{0,6},{1,7},{2,4},{3,5},{4,2},{5,3},{6,0},{7,1},{8,14},{9,15},{10,... | collective-permute-start | bytes 196616 | tf_op jit(solution)/shard_map/ppermute | solution.py:113
  15.0 4.7 %collective-permute-start.5 = (f32[128,128]{1,0:T(8,128)S(1)}, f32[128,128]{1,0:T(8,128)S(1)}, u32[]{:S(2)}, u32[]{:S(2)}) collective-permute-start(f32[128,128]{1,0:T(8,128)S(1)} %add_add_fusion.1), channel_id=1, source_target_pairs={{0,8},{1,9},{2,10},{3,11},{4,12},{5,13},{6,14},{7,15},{8,0},{9,1},... | collective-permute-start | bytes 196616 | tf_op jit(solution)/shard_map/ppermute | solution.py:113
  16.6 6.6 %collective-permute-start.6 = (f32[128,128]{1,0:T(8,128)S(1)}, f32[128,128]{1,0:T(8,128)S(1)}, u32[]{:S(2)}, u32[]{:S(2)}) collective-permute-start(f32[128,128]{1,0:T(8,128)S(1)} %add_add_fusion.1), channel_id=1, source_target_pairs={{0,16},{1,17},{2,18},{3,19},{4,20},{5,21},{6,22},{7,23},{8,24},{9,... | collective-permute-start | bytes 196616 | tf_op jit(solution)/shard_map/ppermute | solution.py:113
  19.2 6.1 %collective-permute-start.7 = (f32[128,128]{1,0:T(8,128)S(1)}, f32[128,128]{1,0:T(8,128)S(1)}, u32[]{:S(2)}, u32[]{:S(2)}) collective-permute-start(f32[128,128]{1,0:T(8,128)S(1)} %add_add_fusion.1), channel_id=1, source_target_pairs={{0,24},{1,25},{2,26},{3,27},{4,28},{5,29},{6,30},{7,31},{8,16},{9,... | collective-permute-start | bytes 196616 | tf_op jit(solution)/shard_map/ppermute | solution.py:113
